TPU v7x, 32 devices: a whole 2x2x4 slice. The times are simulated.
32 devices in a mesh: gx: 4 (over z), gy: 8 (over y, x, core).
Axes of the slice: x: 2, y: 2, z: 4, core: 2. Of those that a mesh axis runs over, the one named last changes fastest.
Arguments:
- tokens: bfloat16 [2048, 7168], P(('gx', 'gy')), may hold values from -6 to 6
- expert_ids: int32 [2048, 8], P(('gx', 'gy')), may hold values from 0 to 95, all different within a row; in each aligned block of 64 rows (0 to 63, 64 to 127, ...) at most 8 rows name the same one
- router_weight: bfloat16 [7168, 96], P(None, ('gx', 'gy')), may hold values from -0.0625 to 0.0625
- gate_weight: bfloat16 [96, 7168, 128], P(('gx', 'gy')), may hold values from -0.0625 to 0.0625
- up_weight: bfloat16 [96, 7168, 128], P(('gx', 'gy')), may hold values from -0.0625 to 0.0625
- down_weight: bfloat16 [96, 128, 7168], P(('gx', 'gy')), may hold values from -0.5 to 0.5
Outputs:
- mixed: bfloat16 [2048, 7168], P(('gx', 'gy'))
Inputs may be any that keep to these rules, and one draw needn't show every extreme that they name: `expert_ids`: each row names 8 different experts of 0 to 95; within each aligned block of 64 rows (the tokens of one device, in order) no expert is named more than 8 times, a bound that some block reaches; every expert is named by some row. Expert e is row e of the expert weight arrays and column e of router_weight.
All inputs are finite; a program needn't handle non-finite values.
Results may differ from a plain program's by a relative error of at most 0.0025.
Values may be sent and summed in bfloat16 or wider, within the bound.
A program may use at most 192 MiB of HBM per device.

v0:
```python
import jax
import jax.numpy as jnp
from jax import lax
from jax.sharding import PartitionSpec as P

route_scale = 2.827
epsilon = 1e-20


def on_whole(shard, axis, dim, block):
    whole = lax.all_gather(shard, axis, axis=dim, tiled=True)
    return block(whole, jnp.int32(0))


def deliver(payload):
    return lax.all_to_all(payload, ("gx", "gy"), split_axis=0, concat_axis=0, tiled=True)


def per_device(tokens, expert_ids, router_weight, gate_weight, up_weight, down_weight):
    count, width = tokens.shape
    top = expert_ids.shape[1]
    local_experts = gate_weight.shape[0]
    devices = lax.axis_size(("gx", "gy"))
    experts = local_experts * devices
    capacity = max(1, (3 * count * top + 2 * experts - 1) // (2 * experts))
    chosen = expert_ids.reshape(-1)
    onehot = (chosen[:, None] == jnp.arange(experts, dtype=jnp.int32)[None, :]).astype(jnp.int32)
    earlier = jnp.cumsum(onehot, axis=0) - onehot
    rank = jnp.sum(earlier * onehot, axis=1)
    slot = chosen * capacity + rank
    owner = jnp.arange(count * top, dtype=jnp.int32) // top
    outgoing = jnp.zeros((experts * capacity, width), tokens.dtype).at[slot].set(tokens[owner])
    arrived = deliver(outgoing.reshape(devices, local_experts * capacity, width))
    arrived = arrived.reshape(devices, local_experts, capacity, width)

    def score_columns(piece, start):
        return jnp.dot(tokens, piece, preferred_element_type=jnp.float32)

    logits = on_whole(router_weight, ("gx", "gy"), 1, score_columns)
    picked = jnp.take_along_axis(jax.nn.sigmoid(logits), expert_ids, axis=1)
    gate = jnp.einsum("nepd,edf->nepf", arrived, gate_weight, preferred_element_type=jnp.float32)
    upper = jnp.einsum("nepd,edf->nepf", arrived, up_weight, preferred_element_type=jnp.float32)
    hidden = (jax.nn.silu(gate) * upper).astype(jnp.bfloat16)
    output = jnp.einsum(
        "nepf,efd->nepd", hidden, down_weight, preferred_element_type=jnp.float32
    ).astype(jnp.bfloat16)
    returned = deliver(output.reshape(devices, local_experts * capacity, width))
    returned = returned.reshape(experts * capacity, width)
    weights = route_scale * picked / (jnp.sum(picked, axis=1, keepdims=True) + epsilon)
    gathered = returned[slot].astype(jnp.float32).reshape(count, top, width)
    mixed = jnp.sum(gathered * weights[:, :, None], axis=1)
    return mixed.astype(jnp.bfloat16)


def solution(mesh):
    placed = (
        P(("gx", "gy"), None),
        P(("gx", "gy"), None),
        P(None, ("gx", "gy")),
        P(("gx", "gy"), None, None),
        P(("gx", "gy"), None, None),
        P(("gx", "gy"), None, None),
    )
    return jax.shard_map(
        per_device, mesh=mesh, in_specs=placed, out_specs=P(("gx", "gy"), None), check_vma=False
    )
```

profile of v0, /device:TPU:1, one launch (start us, length us, event | category | flops | bytes accessed | tf_op | source)
XLA Modules:
  0.0 609.9 jit_solution(14819899962152461888)
XLA Ops:
  6.5 0.0 copy-start
  6.5 0.9 copy.32
  7.4 0.1 eq.29
  7.5 0.1 eq.25
  7.6 0.7 broadcast_multiply_fusion
  8.3 1.3 reduce-window.6
  9.6 0.2 slice_reduce_fusion
  9.8 0.1 copy.31
  9.9 0.1 mul.44
  10.0 0.1 fusion.45
  10.2 0.0 copy-done
  10.2 7.0 %gather_fusion = bf16[512,7168]{1,0:T(8,128)(2,1)} fusion(bf16[64,7168]{1,0:T(8,128)(2,1)S(1)} %copy-done, s32[1024]{0:T(1024)S(1)} %pad_clamp_fusion.1), kind=kCustom, calls=%fused_computation | custom fusion | bytes 14682112 | tf_op jit(solution)/shard_map/gather | solution.py:32
  17.2 19.3 %scatter_custom_fusion = bf16[768,7168]{1,0:T(8,128)(2,1)} fusion(s32[512]{0:T(512)S(1)} %bitcast.88, bf16[512,7168]{1,0:T(8,128)(2,1)} %gather_fusion, bf16[]{:T(256)} %constant.29.clone.1), kind=kCustom, calls=%fused_computation.16 | custom fusion | bytes 11010560 | tf_op jit(solution)/shard_map/scatter | solution.py:32
  36.5 252.4 %all_to_all.10 = bf16[32,24,7168]{2,1,0:T(8,128)(2,1)} all-to-all(bf16[32,24,7168]{2,1,0:T(8,128)(2,1)} %bitcast.85), channel_id=1, replica_groups=mesh['gx'=4,'gy'=8] {'gx','gy'}, dimensions={0} | all-to-all | bytes 22020096 | tf_op jit(solution)/shard_map/all_to_all | solution.py:16
  288.9 7.4 %fusion.11 = f32[32,3,8,128]{3,2,0,1:T(8,128)S(1)} fusion(bf16[3,7168,128]{2,1,0:T(8,128)(2,1)} %param.9, bf16[32,24,7168]{2,1,0:T(8,128)(2,1)} %all_to_all.10), kind=kOutput, calls=%fused_computation.18 | convolution fusion | flops 1409286144 | bytes 16908288 | tf_op jit(solution)/shard_map/nepd,edf->nepf/dot_general | solution.py:41
  296.3 14.2 %fusion.1 = bf16[32,3,8,7168]{3,2,0,1:T(8,128)(2,1)} fusion(bf16[3,128,7168]{2,1,0:T(8,128)(2,1)} %param.11, bf16[3,7168,128]{2,1,0:T(8,128)(2,1)} %param.10, f32[32,3,8,128]{3,2,0,1:T(8,128)S(1)} %fusion.11, bf16[32,24,7168]{2,1,0:T(8,128)(2,1)} %all_to_all.10), kind=kOutput, calls=%fused_computation.8 | convolution fusion | flops 2824667136 | bytes 33423360 | tf_op jit(solution)/shard_map/nepf,efd->nepd/dot_general | solution.py:44
  310.5 9.6 %copy.61 = bf16[32,3,8,7168]{3,2,1,0:T(8,128)(2,1)} copy(bf16[32,3,8,7168]{3,2,0,1:T(8,128)(2,1)} %fusion.1) | data formatting | bytes 22020096 | tf_op jit(solution)/shard_map/convert_element_type | solution.py:46
  320.1 3.6 all-to-all-start.1
  323.7 0.2 all-gather.3.cloned.1.call-start
  324.0 0.5 all-gather.3.cloned.1.call-update
  324.5 0.1 copy.38
  324.6 0.1 reshape.152
  324.7 94.8 %all-gather.3.cloned.1.call-done = bf16[32,3,7168]{2,1,0:T(4,128)(2,1)} async-done(((bf16[1,3,7168]{2,1,0:T(4,128)(2,1)}), bf16[32,3,7168]{2,1,0:T(4,128)(2,1)}) %all-gather.3.cloned.1.call-update) | async-done | bytes 1376272 | tf_op jit(solution)/shard_map/all_gather | solution.py:11
  419.5 3.0 reshape.172
  422.4 0.6 fusion.37
  423.1 3.6 gather_fusion.2
  426.7 0.1 reshape.155
  426.8 0.1 copy.39
  426.9 0.1 copy.40
  427.0 146.5 %all-to-all-done.1 = bf16[32,24,7168]{2,1,0:T(8,128)(2,1)} async-done(((bf16[32,24,7168]{2,1,0:T(8,128)(2,1)}), bf16[32,24,7168]{2,1,0:T(8,128)(2,1)}, u32[]{:S(2)}, u32[]{:S(2)}) %all-to-all-start.1) | async-done | bytes 11010080 | tf_op jit(solution)/shard_map/all_to_all | solution.py:16
  573.5 19.5 %gather_fusion.1 = bf16[512,7168]{1,0:T(8,128)(2,1)} fusion(bf16[768,7168]{1,0:T(8,128)(2,1)} %bitcast.16, s32[1024]{0:T(1024)S(1)} %pad_clamp_fusion), kind=kCustom, calls=%fused_computation.1 | custom fusion | bytes 14682112 | tf_op jit(solution)/shard_map/gather | solution.py:50
  593.0 9.8 %fusion = bf16[64,7168]{1,0:T(8,128)(2,1)} fusion(bf16[512,7168]{1,0:T(8,128)(2,1)} %gather_fusion.1, f32[64,8]{1,0:T(8,128)S(1)} %copy.40), kind=kLoop, calls=%fused_computation.5 | loop fusion | flops 10551296 | bytes 8259584 | tf_op jit(solution)/shard_map/reduce_sum | solution.py:51
  (13 shorter events, 0.1 us)
Async XLA Ops:
  6.5 3.7 copy-start
  320.1 4.4 copy-start.1
  320.1 253.4 %all-to-all-start.1 = ((bf16[32,24,7168]{2,1,0:T(8,128)(2,1)}), bf16[32,24,7168]{2,1,0:T(8,128)(2,1)}, u32[]{:S(2)}, u32[]{:S(2)}) async-start(bf16[32,24,7168]{2,1,0:T(8,128)(2,1)} %bitcast.84), calls=%async_computation.1 | async-start | bytes 22020096 | tf_op jit(solution)/shard_map/all_to_all | solution.py:16
  323.7 95.7 %all-gather.3.cloned.1.call-start = ((), (), s32[]{:S(2)}) async-start(), calls=%async_computation.2 | async-start | bytes 1892352 | tf_op jit(solution)/shard_map/all_gather | solution.py:11
Sparse Core Ops, SparseCore 0:
  327.4 92.0 all-gather.2
where the time goes:
time: 614 us; the launch traced here: 610 us
  blocking collectives  252 us (41%)
  waiting for transfers between devices  242 us (39%)
  local copies, waits for them, and re-layouts  63.8 us (10%)
  matrix products  22.3 us (4%)
  between operations  13.8 us (2%)
  other arithmetic  12 us (2%)
    all_to_all x1, blocking collectives, deliver(): lax.all_to_all(payload, ('gx', 'gy'), split_axis=0, concat_axis=0, tiled=...  252 us
    all_to_all x1, waiting for transfers between devices, deliver(): lax.all_to_all(payload, ('gx', 'gy'), split_axis=0, concat_axis=0, tiled=...  147 us
    all_gather x1, waiting for transfers between devices, on_whole(): whole = lax.all_gather(shard, axis, axis=dim, tiled=True)  94.8 us
    gather x1, local copies, waits for them, and re-layouts, per_device(): gathered = returned[slot].astype(jnp.float32).reshape(count, top, width)  19.5 us
    scatter x1, local copies, waits for them, and re-layouts, per_device(): jnp.zeros((experts * capacity, width), tokens.dtype).at[slot]  19.3 us
    dot_general x1, matrix products, per_device(): jnp.einsum('nepf,efd->nepd', hidden, down_weight, preferred_element_type=...  14.2 us
  transfers between devices with their start and end apart: 2, of which 2 were waited for; matrix products, arithmetic and copies ran while one was open for 1% of the time, Pallas kernels for 0%

commit v1 on v0

v1 whole, which is shorter than its diff:
```python
import jax
import jax.numpy as jnp
from jax import lax
from jax.sharding import PartitionSpec as P

route_scale = 2.827
epsilon = 1e-20
both = ("gx", "gy")


def slots(ids, experts_wanted):
    member = jnp.any(ids[:, None, :, :] == experts_wanted[None, :, None, None], axis=3)
    member = member.astype(jnp.int32)
    rank = jnp.cumsum(member, axis=2) - member
    return member, rank


def per_device(tokens, expert_ids, router_weight, gate_weight, up_weight, down_weight):
    count, width = tokens.shape
    top = expert_ids.shape[1]
    local, _, hidden_width = gate_weight.shape
    devices = lax.axis_size(both)
    experts = local * devices
    capacity = max(1, (3 * count * top + 2 * experts - 1) // (2 * experts))
    rows_of = lax.axis_size("gx")
    columns_of = lax.axis_size("gy")
    here = lax.axis_index("gx")
    part = width // columns_of
    plane = columns_of * local

    all_tokens = lax.all_gather(tokens, both, axis=0, tiled=True)
    sliced = down_weight.reshape(local, hidden_width, columns_of, part).transpose(2, 0, 1, 3)
    down = lax.all_to_all(sliced, "gy", split_axis=0, concat_axis=0, tiled=True)
    all_ids = lax.all_gather(expert_ids, both, axis=0, tiled=False)
    router = lax.all_gather(router_weight.T, both, axis=0, tiled=True)

    near = here * plane + jnp.arange(plane, dtype=jnp.int32)
    member, rank = slots(all_ids, near)
    places = jnp.arange(capacity, dtype=jnp.int32)
    pick = (member[:, :, None, :] > 0) & (rank[:, :, None, :] == places[None, None, :, None])
    own_pick = lax.dynamic_slice_in_dim(pick, lax.axis_index("gy") * local, local, axis=1)

    gate = jnp.einsum("td,edf->tef", all_tokens, gate_weight, preferred_element_type=jnp.float32)
    upper = jnp.einsum("td,edf->tef", all_tokens, up_weight, preferred_element_type=jnp.float32)
    hidden = (jax.nn.silu(gate) * upper).astype(jnp.bfloat16)
    hidden = hidden.reshape(devices, count, local, hidden_width)
    chosen = jnp.einsum(
        "nepc,ncef->enpf", own_pick.astype(jnp.bfloat16), hidden, preferred_element_type=jnp.float32
    ).astype(jnp.bfloat16)
    chosen = lax.all_gather(chosen, "gy", axis=0, tiled=True)
    output = jnp.einsum(
        "enpf,efd->nepd",
        chosen,
        down.reshape(plane, hidden_width, part),
        preferred_element_type=jnp.float32,
    ).astype(jnp.bfloat16).reshape(devices, plane * capacity, part)

    logits = jnp.einsum("td,ed->te", all_tokens, router, preferred_element_type=jnp.float32)
    scores = jax.nn.sigmoid(logits)
    everyone = jnp.arange(experts, dtype=jnp.int32)
    hits = all_ids.reshape(-1, top)[:, :, None] == everyone
    picked = jnp.where(jnp.any(hits, axis=1), scores, 0.0)
    weights = route_scale * picked / (jnp.sum(picked, axis=1, keepdims=True) + epsilon)
    weights = lax.dynamic_slice_in_dim(weights, here * plane, plane, axis=1)
    weights = weights.reshape(devices, count, plane)
    spread = jnp.where(pick.transpose(0, 3, 1, 2), weights[:, :, :, None], 0.0)
    spread = spread.reshape(devices, count, plane * capacity)
    high = lax.reduce_precision(spread, 8, 7)
    middle = lax.reduce_precision(spread - high, 8, 7)
    low = spread - high - middle
    factors = jnp.concatenate([high, middle, low], axis=1).astype(jnp.bfloat16)
    parts = jnp.einsum("nts,nsd->ntd", factors, output, preferred_element_type=jnp.float32)
    partial = jnp.sum(parts.reshape(devices, 3, count, part), axis=1)
    total = lax.psum_scatter(partial.reshape(-1, part), "gx", scatter_dimension=0, tiled=True)
    mixed = total.astype(jnp.bfloat16).reshape(columns_of, count, part)
    mixed = lax.all_to_all(mixed, "gy", split_axis=0, concat_axis=0, tiled=True)
    return mixed.transpose(1, 0, 2).reshape(count, width)


def solution(mesh):
    placed = (
        P(both, None),
        P(both, None),
        P(None, both),
        P(both, None, None),
        P(both, None, None),
        P(both, None, None),
    )
    return jax.shard_map(
        per_device, mesh=mesh, in_specs=placed, out_specs=P(both, None), check_vma=False
    )
```

time: 614 us -> 532 us (0.87)
  blocking collectives: 252 us -> 116 us
  matrix products: 22.3 us -> 81.8 us
  local copies, waits for them, and re-layouts: 63.8 us -> 22.1 us
  waiting for transfers between devices: 242 us -> 264 us
  other arithmetic: 12 us -> 26.9 us
    all_to_all x1, blocking collectives: 252 us -> 17.4 us  [per_device(): mixed = lax.all_to_all(mixed, 'gy', split_axis=0, concat_axis=0, tiled=True)]
    all_to_all x1, waiting for transfers between devices: 147 us -> 0.01 us  [per_device(): down = lax.all_to_all(sliced, 'gy', split_axis=0, concat_axis=0, tiled=True)]
    reduce_scatter x0 -> x1, waiting for transfers between devices: none -> 127 us  [per_device(): lax.psum_scatter(partial.reshape(-1, part), 'gx', scatter_dimension=0, ti...]
    all_gather x0 -> x1, blocking collectives: none -> 98.7 us  [per_device(): all_ids = lax.all_gather(expert_ids, both, axis=0, tiled=False)]
    dot_general x3 -> x6, matrix products: 22.3 us -> 81.8 us  [the longest x1 21.4 us: per_device(): jnp.einsum('td,edf->tef', all_tokens, up_weight, preferred_element_type=j...]
    all_gather x1 -> x3, waiting for transfers between devices: 94.8 us -> 136 us  [the longest x1 133 us: per_device(): all_tokens = lax.all_gather(tokens, both, axis=0, tiled=True)]
    gather x7 -> x0, local copies, waits for them, and re-layouts: 30.4 us -> none  [the longest x1 19.5 us: per_device(): gathered = returned[slot].astype(jnp.float32).reshape(count, top, width)]
    scatter x1 -> x0, local copies, waits for them, and re-layouts: 19.3 us -> none  [per_device(): jnp.zeros((experts * capacity, width), tokens.dtype).at[slot]]
  transfers between devices with their start and end apart: 2 -> 5, of which waited for: 2 -> 3; matrix products, arithmetic and copies ran while one was open for 1% -> 17% of each run, Pallas kernels for 0% -> 0%
where the time goes in v1:
time: 532 us; the launch traced here: 530 us
  waiting for transfers between devices  264 us (50%)
  blocking collectives  116 us (22%)
  matrix products  81.8 us (15%)
  other arithmetic  26.9 us (5%)
  local copies, waits for them, and re-layouts  22.1 us (4%)
  between operations  13.3 us (2%)
  starting transfers between devices  5.62 us (1%)
    all_gather x1, waiting for transfers between devices, per_device(): all_tokens = lax.all_gather(tokens, both, axis=0, tiled=True)  133 us
    reduce_scatter x1, waiting for transfers between devices, per_device(): lax.psum_scatter(partial.reshape(-1, part), 'gx', scatter_dimension=0, ti...  127 us
    all_gather x1, blocking collectives, per_device(): all_ids = lax.all_gather(expert_ids, both, axis=0, tiled=False)  98.7 us
    dot_general x1, matrix products, per_device(): jnp.einsum('td,edf->tef', all_tokens, up_weight, preferred_element_type=j...  21.4 us
    dot_general x1, matrix products, per_device(): jnp.einsum('td,edf->tef', all_tokens, gate_weight, preferred_element_type...  20.5 us
    all_to_all x1, blocking collectives, per_device(): mixed = lax.all_to_all(mixed, 'gy', split_axis=0, concat_axis=0, tiled=True)  17.4 us
    dot_general x1, matrix products, per_device(): jnp.einsum('td,ed->te', all_tokens, router, preferred_element_type=jnp.fl...  14.6 us
    dot_general x1, matrix products, per_device(): jnp.einsum('nts,nsd->ntd', factors, output, preferred_element_type=jnp.fl...  14.1 us
  transfers between devices with their start and end apart: 5, of which 3 were waited for; matrix products, arithmetic and copies ran while one was open for 17% of the time, Pallas kernels for 0%

profile of v1, /device:TPU:1, one launch (start us, length us, event | category | flops | bytes accessed | tf_op | source)
XLA Modules:
  0.0 530.1 jit_solution(8671563799331421305)
XLA Ops:
  6.5 0.7 all-gather.11.cloned.1.call-update
  7.3 0.7 all-gather.7.cloned.1.call-update
  8.0 5.9 %copy.62 = bf16[3,16,8,8,896]{4,3,1,0,2:T(8,128)(2,1)} copy(bf16[3,16,8,8,896]{4,3,2,1,0:T(8,128)(2,1)} %bitcast.58) | data formatting | bytes 11010048 | tf_op jit(solution)/shard_map/reshape | solution.py:32
  13.9 5.4 %all-to-all-start = ((bf16[8,3,128,896]{3,2,1,0:T(8,128)(2,1)}), bf16[8,3,128,896]{3,2,1,0:T(8,128)(2,1)}, u32[]{:S(2)}, u32[]{:S(2)}) async-start(bf16[8,3,128,896]{3,2,1,0:T(8,128)(2,1)} %bitcast.57), calls=%async_computation | async-start | bytes 11010048 | tf_op jit(solution)/shard_map/all_to_all | solution.py:33
  19.3 98.7 %all-gather.1 = s32[32,64,8]{1,2,0:T(8,128)S(1)} all-gather(s32[1,64,8]{1,2,0:T(8,128)S(1)} %bitcast.64), channel_id=2, replica_groups=mesh['gx'=4,'gy'=8] {'gx','gy'}, dimensions={0}, use_global_device_ids=true | all-gather | bytes 67584 | tf_op jit(solution)/shard_map/all_gather | solution.py:34
  118.1 0.7 reshape.67
  118.8 1.2 compare_reduce_fusion
  120.1 0.7 copy.49
  120.7 7.1 %reduce_window_sum.11 = s32[32,24,64]{2,1,0:T(8,128)S(1)} reduce-window(s32[32,24,64]{2,1,0:T(8,128)S(1)} %get-tuple-element.11, s32[]{:T(128)} %constant.6.clone.1), window={size=1x1x64 pad=0_0x0_0x63_0}, to_apply=%region_1.0 | reduce-window | flops 3096576 | bytes 393220 | tf_op jit(solution)/shard_map/jit(cumsum)/reduce_window_sum | solution.py:14
  127.9 0.8 copy.50
  129.1 2.0 copy.45
  131.5 2.5 copy.44
  134.0 0.7 constant_dynamic-slice_fusion.1
  134.7 0.8 constant_dynamic-slice_fusion
  135.5 1.1 fusion.7
  136.6 3.0 reshape.69
  139.6 133.3 %all-gather.7.cloned.1.call-done = bf16[2048,7168]{1,0:T(8,128)(2,1)} async-done(((bf16[64,7168]{1,0:T(8,128)(2,1)}), bf16[2048,7168]{1,0:T(8,128)(2,1)}) %all-gather.7.cloned.1.call-update) | async-done | bytes 29360144 | tf_op jit(solution)/shard_map/all_gather | solution.py:31
  272.8 20.5 %fusion.2 = f32[2048,3,128]{2,0,1:T(8,128)S(1)} fusion(bf16[3,7168,128]{2,1,0:T(8,128)(2,1)} %param.9, bf16[2048,7168]{1,0:T(8,128)(2,1)} %all-gather.7.cloned.1.call-done), kind=kOutput, calls=%fused_computation.2 | convolution fusion | flops 11274289152 | bytes 38010880 | tf_op jit(solution)/shard_map/td,edf->tef/dot_general | solution.py:43
  293.3 21.4 %multiply_convert_fusion = bf16[2048,3,128]{2,0,1:T(8,128)(2,1)S(1)} fusion(f32[2048,3,128]{2,0,1:T(8,128)S(1)} %fusion.2, bf16[3,7168,128]{2,1,0:T(8,128)(2,1)} %param.10, bf16[2048,7168]{1,0:T(8,128)(2,1)} %all-gather.7.cloned.1.call-done), kind=kOutput, calls=%fused_computation.16 | convolution fusion | flops 11279007744 | bytes 39583744 | tf_op jit(solution)/shard_map/td,edf->tef/dot_general | solution.py:44
  314.7 1.2 convolution_convert_fusion
  316.2 14.6 %fusion.27 = (f32[2048]{0:T(1024)S(1)}, f32[2048,96]{0,1:T(8,128)S(1)}) fusion(pred[2048,96]{0,1:T(8,128)(4,1)S(1)} %fusion.7, bf16[2048,7168]{1,0:T(8,128)(2,1)} %all-gather.7.cloned.1.call-done, bf16[96,7168]{1,0:T(8,128)(2,1)S(1)} %reshape.69), kind=kOutput, calls=%fused_computation.47 | convolution fusion | flops 2819553280 | bytes 31727616 | tf_op jit(solution)/shard_map/td,ed->te/dot_general | solution.py:58
  331.6 2.4 copy.48
  334.0 3.0 reduce-precision_convert_fusion.1
  337.1 0.5 reduce-precision_convert_fusion
  337.6 2.5 all-gather.9.cloned.1.call-done
  340.0 10.1 %convert_bitcast_fusion = bf16[32,24,8,896]{3,2,0,1:T(8,128)(2,1)} fusion(bf16[24,32,8,128]{3,2,1,0:T(8,128)(2,1)} %all-gather.9.cloned.1.call-done, bf16[24,128,896,1]{2,1,3,0:T(8,128)(2,1)} %bitcast.13), kind=kOutput, calls=%fused_computation.7 | convolution fusion | flops 1414791168 | bytes 18087936 | tf_op jit(solution)/shard_map/enpf,efd->nepd/dot_general | solution.py:51
  350.1 14.1 %fusion.4 = f32[32,192,896]{2,1,0:T(8,128)} fusion(bf16[32,24,8,896]{3,2,0,1:T(8,128)(2,1)} %convert_bitcast_fusion, bf16[32,64,192]{2,1,0:T(8,128)(2,1)S(1)} %get-tuple-element.8, bf16[32,64,192]{2,1,0:T(8,128)(2,1)S(1)} %get-tuple-element.7, bf16[32,64,192]{2,1,0:T(8,128)(2,1)S(1)} %get-tuple-element.5), kind=kOutput, calls=%fused_computation.4 | convolution fusion | flops 2121007104 | bytes 35389440 | tf_op jit(solution)/shard_map/nts,nsd->ntd/dot_general | solution.py:72
  364.2 12.2 %reduce_sum.19 = f32[32,64,896]{2,1,0:T(8,128)} reduce(f32[32,3,64,896]{3,2,1,0:T(8,128)} %bitcast.55, f32[]{:T(128)} %constant.7.clone.1), dimensions={1}, to_apply=%region_4.5 | reduce | flops 3670016 | bytes 29360132 | tf_op jit(solution)/shard_map/reduce_sum | solution.py:73
  376.5 127.1 %reduce-scatter.2.cloned.1.call-done = f32[512,896]{1,0:T(8,128)} async-done(((f32[2048,896]{1,0:T(8,128)}), f32[512,896]{1,0:T(8,128)}) %reduce-scatter.2.cloned.1.call-update) | async-done | bytes 1835024 | tf_op jit(solution)/shard_map/reduce_scatter | solution.py:74
  503.5 1.6 convert_element_type.39
  505.1 17.4 %all_to_all.10 = bf16[8,64,896]{2,1,0:T(8,128)(2,1)S(1)} all-to-all(bf16[8,64,896]{2,1,0:T(8,128)(2,1)S(1)} %bitcast.60), channel_id=1, replica_groups=mesh['gx'=4,'gy'=8] {'gy'}, dimensions={0} | all-to-all | bytes 1835008 | tf_op jit(solution)/shard_map/all_to_all | solution.py:76
  522.5 1.1 copy.56
  (25 shorter events, 2.1 us)
Async XLA Ops:
  6.5 130.0 %all-gather.11.cloned.1.call-start = ((), (), s32[]{:S(2)}) async-start(), calls=%async_computation.6 | async-start | bytes 1892352 | tf_op jit(solution)/shard_map/all_gather | solution.py:35
  7.3 265.6 %all-gather.7.cloned.1.call-start = ((), (), s32[]{:S(2)}) async-start(), calls=%async_computation.3 | async-start | bytes 30277632 | tf_op jit(solution)/shard_map/all_gather | solution.py:31
  13.9 5.5 %copy-start.1 = (s32[64,8]{0,1:T(8,128)S(1)}, s32[64,8]{0,1:T(8,128)}, u32[]{:S(2)}) copy-start(s32[64,8]{0,1:T(8,128)} %param.7) | copy-start | bytes 6148
  13.9 323.7 %all-to-all-start = ((bf16[8,3,128,896]{3,2,1,0:T(8,128)(2,1)}), bf16[8,3,128,896]{3,2,1,0:T(8,128)(2,1)}, u32[]{:S(2)}, u32[]{:S(2)}) async-start(bf16[8,3,128,896]{3,2,1,0:T(8,128)(2,1)} %bitcast.57), calls=%async_computation | async-start | bytes 11010048 | tf_op jit(solution)/shard_map/all_to_all | solution.py:33
  19.2 320.8 %all-gather.9.cloned.1.call-start = ((), (), s32[]{:S(2)}) async-start(), calls=%async_computation.4 | async-start | bytes 1769472 | tf_op jit(solution)/shard_map/all_gather | solution.py:50
  131.5 4.0 copy-start
  315.9 187.6 %reduce-scatter.2.cloned.1.call-start = ((), (), s32[]{:S(2)}) async-start(), calls=%async_computation.5 | async-start | bytes 9175040 | tf_op jit(solution)/shard_map/reduce_scatter | solution.py:74
Sparse Core Ops, SparseCore 0:
  10.2 87.3 all-gather.10
  100.4 172.4 all-gather.6
  316.0 23.9 all-gather.8
  376.6 126.8 reduce-scatter.1
